TPU v7x, 32 devices: a whole 2x2x4 slice. The times are simulated.
32 devices in a mesh: grp: 2 (over core), dp: 4 (over z), mp: 4 (over y, x).
Axes of the slice: x: 2, y: 2, z: 4, core: 2. Of those that a mesh axis runs over, the one named last changes fastest.
Arguments:
- hidden: bfloat16 [1024, 5120], P(('dp', 'mp')), may hold values from -6 to 6
- enc_weight: bfloat16 [5120, 8192], P(None, 'mp'), may hold values from -0.078125 to 0.078125
- enc_bias: bfloat16 [8192], P('mp'), may hold values from -5 to 5
- enc_frozen: bfloat16 [5120, 64], replicated, may hold values from -0.078125 to 0.078125
- enc_adapter: bfloat16 [64, 8192], P(None, 'mp'), may hold values from -0.75 to 0.75
- text_rows: bfloat16 [2560, 8192], P(('dp', 'mp')), may hold values from -6 to 6
- norm_gain: bfloat16 [8192], replicated, may hold values from 0.5 to 1.5
- value_weight: bfloat16 [8192, 1024], P(('dp', 'mp')), may hold values from -0.0625 to 0.0625
- value_bias: bfloat16 [1024], replicated, may hold values from -5 to 5
- llm_frozen: bfloat16 [8192, 64], P(('dp', 'mp')), may hold values from -0.0625 to 0.0625
- llm_adapter: bfloat16 [64, 1024], replicated, may hold values from -0.75 to 0.75
- targets: bfloat16 [2560, 1024], P(('dp', 'mp')), may hold values from -6 to 6
- dest_owner: int32 [1024, 1], replicated, may hold values from 0 to 15; in each aligned block of 256 rows (0 to 255, 256 to 511, ...) at most 32 rows name the same one
- seq_length: int32 [16], P(('dp', 'mp')), may hold values from 128 to 160
Outputs:
- grad_enc: float32 [64, 8192], P('grp', 'mp')
- grad_llm: float32 [64, 1024], P('grp')
Inputs may be any that keep to these rules, and one draw needn't show every extreme that they name: `dest_owner`: within the tokens of one encoder block (aligned blocks of 256 rows) no LLM device is named more than 32 times, and some device is named exactly 32 times in some blocks.
All inputs are finite; a program needn't handle non-finite values.
Results may differ from a plain program's by a relative error of at most 0.003.
Values may be sent and summed in bfloat16 or wider, within the bound.
A program may use at most 128 MiB of HBM per device.

v0:
```python
import jax
import jax.numpy as jnp
from jax import lax
from jax.sharding import PartitionSpec as P

ENC_DEV = 256
epsilon = 1e-06


def passed_along(value, axis, steps):
    count = lax.axis_size(axis)
    first, last = (max(0, -steps), min(count, count - steps))
    return lax.ppermute(value, axis, [(source, source + steps) for source in range(first, last)])


def swapped(array, axis, bit):
    return lax.ppermute(array, axis, [(i, i ^ 1 << bit) for i in range(lax.axis_size(axis))])


def slot_ranks(destiny, owners):
    markers = (destiny[:, None] == jnp.arange(owners, dtype=jnp.int32)[None, :]).astype(jnp.int32)
    return jnp.sum((jnp.cumsum(markers, axis=0) - markers) * markers, axis=1)


def body(
    hidden,
    enc_weight,
    enc_bias,
    enc_frozen,
    enc_adapter,
    text_rows,
    norm_gain,
    value_weight,
    value_bias,
    llm_frozen,
    llm_adapter,
    targets,
    dest_owner,
    seq_length,
):
    data_ways = lax.axis_size("dp")
    model_ways = lax.axis_size("mp")
    owners = data_ways * model_ways
    capacity = 2 * ENC_DEV // owners
    area = capacity * data_ways
    encoder = lax.axis_index("grp") == 0
    data_index = lax.axis_index("dp")
    owner_index = data_index * model_ways + lax.axis_index("mp")
    part_width = enc_weight.shape[1]
    rank_width = enc_frozen.shape[1]
    kv_width = llm_adapter.shape[1]
    group_rows = lax.all_gather(hidden, "mp", axis=0, tiled=True)

    def encode(source):
        low_rank = jnp.dot(source, enc_frozen, preferred_element_type=jnp.float32).astype(
            jnp.bfloat16
        )
        merged = jnp.dot(source, enc_weight, preferred_element_type=jnp.float32) + enc_bias.astype(
            jnp.float32
        )
        merged = merged + jnp.dot(low_rank, enc_adapter, preferred_element_type=jnp.float32)
        return (merged.astype(jnp.bfloat16), low_rank)

    def rest_encode(source):
        return (
            jnp.zeros((source.shape[0], part_width), jnp.bfloat16),
            jnp.zeros((source.shape[0], rank_width), jnp.bfloat16),
        )

    merged_rows, enc_low = lax.cond(encoder, encode, rest_encode, group_rows)
    destiny = dest_owner[:, 0]
    own_dest = lax.dynamic_slice_in_dim(destiny, data_index * ENC_DEV, ENC_DEV)
    bucket_index = slot_ranks(own_dest, owners) * owners + own_dest
    outgoing = (
        jnp.zeros((capacity * owners, part_width), jnp.bfloat16).at[bucket_index].set(merged_rows)
    )
    outgoing = outgoing.reshape(capacity, owners, part_width)
    grouped = lax.all_to_all(outgoing, ("dp", "mp"), split_axis=1, concat_axis=1, tiled=True)
    arrived = passed_along(grouped, "grp", 1)
    counts = jnp.sum((destiny.reshape(data_ways, ENC_DEV) == owner_index).astype(jnp.int32), axis=1)
    usable = (jnp.arange(capacity, dtype=jnp.int32)[:, None] < counts[None, :]).reshape(area, 1)
    gathered = (
        lax.all_gather(value_weight, ("dp", "mp"), axis=0, tiled=True),
        lax.all_gather(llm_frozen, ("dp", "mp"), axis=0, tiled=True),
    )

    def learn_layer(operands):
        incoming, whole_value, whole_frozen = operands
        image_rows = incoming.reshape(area, -1)
        head_rows = jnp.where(usable, image_rows, text_rows[:area])
        all_rows = jnp.concatenate([head_rows, text_rows[area:]], axis=0)
        wide_rows = all_rows.astype(jnp.float32)
        inverse = lax.rsqrt(jnp.mean(wide_rows * wide_rows, axis=1, keepdims=True) + epsilon)
        gain_wide = norm_gain.astype(jnp.float32)
        normed = (wide_rows * inverse * gain_wide).astype(jnp.bfloat16)
        low_rank = jnp.dot(normed, whole_frozen, preferred_element_type=jnp.float32).astype(
            jnp.bfloat16
        )
        values_out = jnp.dot(
            normed, whole_value, preferred_element_type=jnp.float32
        ) + value_bias.astype(jnp.float32)
        values_out = values_out + jnp.dot(low_rank, llm_adapter, preferred_element_type=jnp.float32)
        length = seq_length[0]
        position = jnp.arange(all_rows.shape[0], dtype=jnp.int32)
        row_weight = jnp.where(position < length, 1.0 / length.astype(jnp.float32), 0.0)
        dvalues = ((values_out - targets.astype(jnp.float32)) * row_weight[:, None]).astype(
            jnp.bfloat16
        )
        grad_part = jnp.dot(low_rank.T, dvalues, preferred_element_type=jnp.float32)
        head_dv = dvalues[:area]
        low_grad = jnp.dot(head_dv, llm_adapter.T, preferred_element_type=jnp.float32).astype(
            jnp.bfloat16
        )
        dnormed = jnp.dot(head_dv, whole_value.T, preferred_element_type=jnp.float32)
        dnormed = dnormed + jnp.dot(low_grad, whole_frozen.T, preferred_element_type=jnp.float32)
        scaled = gain_wide * dnormed
        head_wide = wide_rows[:area]
        head_inverse = inverse[:area]
        cubed = head_inverse * head_inverse * head_inverse
        image_grad = head_inverse * scaled - head_wide * cubed * jnp.mean(
            scaled * head_wide, axis=1, keepdims=True
        )
        image_grad = image_grad.astype(jnp.bfloat16)
        reply_rows = jnp.where(usable, image_grad, jnp.zeros_like(image_grad))
        return (grad_part, reply_rows.reshape(capacity, owners, part_width))

    def rest_learn(operands):
        return (
            jnp.zeros((rank_width, kv_width), jnp.float32),
            jnp.zeros((capacity, owners, part_width), jnp.bfloat16),
        )

    llm_part, reply_rows = lax.cond(
        encoder, rest_learn, learn_layer, (arrived, gathered[0], gathered[1])
    )
    llm_total = lax.psum(llm_part, ("dp", "mp"))
    grouped_back = lax.all_to_all(reply_rows, ("dp", "mp"), split_axis=1, concat_axis=1, tiled=True)
    returned = passed_along(grouped_back, "grp", -1)

    def adapt_grad(operands):
        back_rows, low_rank = operands
        image_grad = back_rows.reshape(capacity * owners, part_width)[bucket_index]
        return jnp.dot(low_rank.T, image_grad, preferred_element_type=jnp.float32)

    def rest_adapt(operands):
        return jnp.zeros((rank_width, part_width), jnp.float32)

    enc_part = lax.cond(encoder, adapt_grad, rest_adapt, (returned, enc_low))
    enc_total = lax.psum(enc_part, "dp")
    half_rank = rank_width // 2
    enc_count = half_rank * part_width
    llm_count = half_rank * kv_width
    span = max(enc_count, llm_count)
    enc_upper = enc_total[half_rank:].reshape(-1)
    llm_lower = jnp.pad(llm_total[:half_rank].reshape(-1), (0, span - llm_count))
    sending = jnp.where(encoder, enc_upper, llm_lower)
    received = swapped(sending, "grp", 0)
    grad_enc = jnp.where(encoder, enc_total[:half_rank], received.reshape(half_rank, part_width))
    grad_llm = jnp.where(
        encoder, received[:llm_count].reshape(half_rank, kv_width), llm_total[half_rank:]
    )
    return (grad_enc, grad_llm)


def solution(mesh):
    return jax.shard_map(
        body,
        mesh=mesh,
        in_specs=(
            P(("dp", "mp"), None),
            P(None, "mp"),
            P("mp"),
            P(),
            P(None, "mp"),
            P(("dp", "mp"), None),
            P(),
            P(("dp", "mp"), None),
            P(),
            P(("dp", "mp"), None),
            P(),
            P(("dp", "mp"), None),
            P(),
            P(("dp", "mp")),
        ),
        out_specs=(P("grp", "mp"), P("grp", None)),
        check_vma=False,
    )
```

profile of v0, /device:TPU:0, one launch (start us, length us, event | category | flops | bytes accessed | tf_op | source)
XLA Modules:
  0.0 564.6 jit_solution(298686897474769356)
XLA Ops:
  7.9 1.6 copy.49
  12.6 39.5 %all-gather.4.cloned.1.call-done = bf16[256,5120]{1,0:T(8,128)(2,1)} async-done(((bf16[64,5120]{1,0:T(8,128)(2,1)}), bf16[256,5120]{1,0:T(8,128)(2,1)}) %all-gather.4.cloned.1.call-update) | async-done | bytes 2621456 | tf_op jit(solution)/shard_map/all_gather | solution.py:52
  52.1 15.1 %conditional.3 = (bf16[256,2048]{1,0:T(8,128)(2,1)S(1)}, bf16[256,64]{0,1:T(8,128)(2,1)}) conditional(s32[]{:T(128)} %convert_element_type.60, () %tuple.31, (bf16[256,5120]{1,0:T(8,128)(2,1)}, bf16[5120,2048]{1,0:T(8,128)(2,1)}, bf16[2048]{0:T(1024)(128)(2,1)}, bf16[5120,64]{0,1:T(8,128)(2,1)}, bf16[64,2048]{1,0:T(8,128)(2,1)}) %tuple.32), branch_computations={%region_3.4_spmd, %region_4.5_spmd} | conditional | flops 5605181440 | bytes 44011620 | solution.py:70
  52.1 3.6 convolution_convert_fusion
  55.7 1.2 fusion.21
  56.9 10.3 %fusion.1 = bf16[256,2048]{1,0:T(8,128)(2,1)S(1)} fusion(f32[256,2048]{1,0:T(8,128)S(1)} %fusion.21, bf16[256,5120]{1,0:T(8,128)(2,1)S(1)} %copy-done.1, bf16[5120,2048]{1,0:T(8,128)(2,1)} %get-tuple-element.87, f32[2048]{0:T(1024)S(1)} %convert_element_type.42), kind=kOutput, calls=%fused_computation.4 | convolution fusion | flops 5370281984 | bytes 26746880 | tf_op jit(solution)/shard_map/cond/branch_1_fun/dot_general | solution.py:58
  68.2 3.5 scatter_custom_fusion
  71.7 1.2 copy.48
  72.9 59.7 %all_to_all.10 = bf16[32,16,2048]{2,0,1:T(8,128)(2,1)} all-to-all(bf16[32,16,2048]{2,0,1:T(8,128)(2,1)S(1)} %copy.48), channel_id=1, replica_groups=mesh['grp'=2,'dp'=4,'mp'=4] {'dp','mp'}, dimensions={1} | all-to-all | bytes 4194304 | tf_op jit(solution)/shard_map/all_to_all | solution.py:78
  132.6 1.4 collective-permute-start
  134.1 3.8 collective-permute-done
  137.9 183.1 %all-gather.8.cloned.1.call-done = bf16[8192,1024]{1,0:T(8,128)(2,1)} async-done(((bf16[512,1024]{1,0:T(8,128)(2,1)}), bf16[8192,1024]{1,0:T(8,128)(2,1)}) %all-gather.8.cloned.1.call-update) | async-done | bytes 16777232 | tf_op jit(solution)/shard_map/all_gather | solution.py:83
  321.6 1.2 copy.51
  322.8 31.6 %all_to_all.11 = bf16[32,16,2048]{2,0,1:T(8,128)(2,1)} all-to-all(bf16[32,16,2048]{2,0,1:T(8,128)(2,1)S(1)} %copy.51), channel_id=1, replica_groups=mesh['grp'=2,'dp'=4,'mp'=4] {'dp','mp'}, dimensions={1} | all-to-all | bytes 4194304 | tf_op jit(solution)/shard_map/all_to_all | solution.py:137
  354.3 1.3 collective-permute-start.1
  355.7 56.2 %collective-permute-done.1 = bf16[32,16,2048]{2,0,1:T(8,128)(2,1)S(1)} collective-permute-done((bf16[32,16,2048]{2,0,1:T(8,128)(2,1)}, bf16[32,16,2048]{2,0,1:T(8,128)(2,1)S(1)}, u32[]{:S(2)}, u32[]{:S(2)}) %collective-permute-start.1) | collective-permute-done | bytes 2097184 | tf_op jit(solution)/shard_map/ppermute | solution.py:13
  411.9 6.5 %conditional.5 = (f32[64,2048]{1,0:T(8,128)S(1)}) conditional(s32[]{:T(128)} %convert_element_type.60, () %tuple.30, (bf16[32,16,2048]{2,0,1:T(8,128)(2,1)S(1)}, s32[256]{0:T(256)S(1)}, s32[256]{0:T(256)S(1)}, bf16[256,64]{0,1:T(8,128)(2,1)}) %tuple.70), branch_computations={%region_11.12_spmd, %region_12.13_spmd} | conditional | flops 67111168 | bytes 16294948 | solution.py:148
  411.9 1.3 copy-done.3
  413.3 2.7 copy.52
  416.0 1.4 gather_fusion
  417.4 1.1 convolution_bitcast_fusion
  419.3 94.8 %all-reduce.6.cloned.1.call-done = f32[64,1024]{1,0:T(8,128)} async-done(((f32[64,1024]{1,0:T(8,128)}), f32[64,1024]{1,0:T(8,128)}) %all-reduce.6.cloned.1.call-update) | async-done | bytes 262160 | tf_op jit(solution)/shard_map/psum | solution.py:136
  515.1 38.7 %all-reduce.4.cloned.1.call-done = f32[64,2048]{1,0:T(8,128)} async-done(((f32[64,2048]{1,0:T(8,128)}), f32[64,2048]{1,0:T(8,128)}) %all-reduce.4.cloned.1.call-update) | async-done | bytes 524304 | tf_op jit(solution)/shard_map/psum | solution.py:149
  555.0 1.5 collective-permute-done.2
  (65 shorter events, 10.2 us)
Async XLA Ops:
  7.2 44.9 %all-gather.4.cloned.1.call-start = ((), (), s32[]{:S(2)}) async-start(), calls=%async_computation.2 | async-start | bytes 3276800 | tf_op jit(solution)/shard_map/all_gather | solution.py:52
  7.9 126.2 %all-gather.6.cloned.1.call-start = ((), (), s32[]{:S(2)}) async-start(), calls=%async_computation.3 | async-start | bytes 2228224 | tf_op jit(solution)/shard_map/all_gather | solution.py:84
  9.6 311.5 %all-gather.8.cloned.1.call-start = ((), (), s32[]{:S(2)}) async-start(), calls=%async_computation.4 | async-start | bytes 17825792 | tf_op jit(solution)/shard_map/all_gather | solution.py:83
  10.3 503.8 %all-reduce.6.cloned.1.call-start = ((), (), s32[]{:S(2)}) async-start(), calls=%async_computation.6 | async-start | bytes 524288 | tf_op jit(solution)/shard_map/psum | solution.py:136
  52.1 3.6 copy-start.11
  52.1 4.8 copy-start.15
  52.1 4.8 copy-start.1
  67.2 1.0 copy-start.6
  72.9 248.2 %copy-start.8 = (bf16[64,1024]{1,0:T(8,128)(2,1)S(1)}, bf16[64,1024]{1,0:T(8,128)(2,1)}, u32[]{:S(2)}) copy-start(bf16[64,1024]{1,0:T(8,128)(2,1)} %param.30) | copy-start | bytes 393220
  72.9 248.2 %copy-start.10 = (bf16[160,1024]{1,0:T(8,128)(2,1)S(1)}, bf16[160,1024]{1,0:T(8,128)(2,1)}, u32[]{:S(2)}) copy-start(bf16[160,1024]{1,0:T(8,128)(2,1)} %param.31) | copy-start | bytes 983044
  72.9 248.2 %copy-start.13 = (bf16[8192]{0:T(1024)(128)(2,1)S(1)}, bf16[8192]{0:T(1024)(128)(2,1)}, u32[]{:S(2)}) copy-start(bf16[8192]{0:T(1024)(128)(2,1)} %param.26) | copy-start | bytes 49156
  72.9 248.2 %copy-start.14 = (s32[1024,1]{0,1:T(1,128)S(1)}, s32[1024,1]{0,1:T(1,128)}, u32[]{:S(2)}) copy-start(s32[1024,1]{0,1:T(1,128)} %param.32) | copy-start | bytes 12292
  72.9 248.2 %copy-start.16 = (bf16[1024]{0:T(1024)(128)(2,1)S(1)}, bf16[1024]{0:T(1024)(128)(2,1)}, u32[]{:S(2)}) copy-start(bf16[1024]{0:T(1024)(128)(2,1)} %param.28) | copy-start | bytes 6148
  132.6 5.3 collective-permute-start
  321.6 32.8 %copy-start.7 = (f32[64,1024]{1,0:T(8,128)}, f32[64,1024]{1,0:T(8,128)S(1)}, u32[]{:S(2)}) copy-start(f32[64,1024]{1,0:T(8,128)S(1)} %get-tuple-element.82) | copy-start | bytes 786436
  354.3 57.6 %collective-permute-start.1 = (bf16[32,16,2048]{2,0,1:T(8,128)(2,1)}, bf16[32,16,2048]{2,0,1:T(8,128)(2,1)S(1)}, u32[]{:S(2)}, u32[]{:S(2)}) collective-permute-start(bf16[32,16,2048]{2,0,1:T(8,128)(2,1)} %all_to_all.11), channel_id=1, source_target_pairs={{16,0},{17,1},{18,2},{19,3},{20,4},{21,5},{22,6},{23,7},{24,8},{25... | collective-permute-start | bytes 6291464 | tf_op jit(solution)/shard_map/ppermute | solution.py:13
  355.7 198.1 %all-reduce.4.cloned.1.call-start = ((), (), s32[]{:S(2)}) async-start(), calls=%async_computation.5 | async-start | bytes 1048576 | tf_op jit(solution)/shard_map/psum | solution.py:149
  411.9 1.3 copy-start.3
  418.5 0.8 copy-start.4
  514.1 43.3 %copy-start.12 = (f32[64,1024]{1,0:T(8,128)S(1)}, f32[64,1024]{1,0:T(8,128)}, u32[]{:S(2)}) copy-start(f32[64,1024]{1,0:T(8,128)} %all-reduce.6.cloned.1.call-done) | copy-start | bytes 786436
  553.8 2.8 copy-start.9
  554.9 1.6 collective-permute-start.2
Sparse Core Ops, SparseCore 0:
  9.8 42.2 all-gather.3
  55.5 72.8 all-gather.5
  131.1 189.8 all-gather.7
  355.8 158.2 all-reduce.5
  516.3 37.5 all-reduce.3
where the time goes:
time: 565 us
  waiting for transfers between devices  419 us (74%)
  blocking collectives  91.3 us (16%)
  local copies, waits for them, and re-layouts  18 us (3%)
  matrix products  16.1 us (3%)
  between operations  14 us (2%)
    all_gather x1, waiting for transfers between devices, body(): lax.all_gather(value_weight, ('dp', 'mp'), axis=0, tiled=True)  183 us
    psum x1, waiting for transfers between devices, body(): llm_total = lax.psum(llm_part, ('dp', 'mp'))  94.8 us
    ppermute x2, waiting for transfers between devices, passed_along(): lax.ppermute(value, axis, [(source, source + steps) for source in range(f...  60 us
    all_to_all x1, blocking collectives, body(): lax.all_to_all(outgoing, ('dp', 'mp'), split_axis=1, concat_axis=1, tiled...  59.7 us
    all_gather x1, waiting for transfers between devices, body(): group_rows = lax.all_gather(hidden, 'mp', axis=0, tiled=True)  39.5 us
    psum x1, waiting for transfers between devices, body(): enc_total = lax.psum(enc_part, 'dp')  38.7 us
    all_to_all x1, blocking collectives, body(): lax.all_to_all(reply_rows, ('dp', 'mp'), split_axis=1, concat_axis=1, til...  31.6 us
  transfers between devices with their start and end apart: 8, of which 7 were waited for; matrix products, arithmetic and copies ran while one was open for 5% of the time, Pallas kernels for 0%

commit v1 on v0

--- a/solution.py
+++ b/solution.py
@@ -1,3 +1,4 @@
+import functools
 import jax
 import jax.numpy as jnp
 from jax import lax
@@ -5,6 +6,21 @@
 
 ENC_DEV = 256
 epsilon = 1e-06
+
+
+def switch_point(mat, chip_axis, out_dim):
+    slots = lax.axis_size(chip_axis)
+    sides = [(pp, (pp + 1) % slots) for pp in range(slots)]
+    b_now = [None] * slots
+    b_now[slots - 1] = mat
+    for h in range(slots - 2, -1, -1):
+        b_now[h] = lax.ppermute(b_now[h + 1], chip_axis, sides)
+    then = jnp.concatenate(b_now, axis=out_dim)
+    heard = (lax.axis_index(chip_axis) + 1) * mat.shape[out_dim]
+    return jnp.roll(then, heard, axis=out_dim)
+
+
+settle_the_screen = functools.partial(switch_point, chip_axis="mp", out_dim=0)
 
 
 def passed_along(value, axis, steps):
@@ -49,7 +65,7 @@
     part_width = enc_weight.shape[1]
     rank_width = enc_frozen.shape[1]
     kv_width = llm_adapter.shape[1]
-    group_rows = lax.all_gather(hidden, "mp", axis=0, tiled=True)
+    group_rows = settle_the_screen(hidden)
 
     def encode(source):
         low_rank = jnp.dot(source, enc_frozen, preferred_element_type=jnp.float32).astype(

time: 565 us -> 542 us (0.959)
  waiting for transfers between devices: 419 us -> 388 us
    ppermute x0 -> x3, waiting for transfers between devices: none -> 50.8 us  [switch_point(): b_now[h] = lax.ppermute(b_now[h + 1], chip_axis, sides)]
    all_gather x1, waiting for transfers between devices: 183 us -> 141 us  [body(): lax.all_gather(value_weight, ('dp', 'mp'), axis=0, tiled=True)]
    all_gather x1 -> x0, waiting for transfers between devices: 39.5 us -> none  [body(): group_rows = lax.all_gather(hidden, 'mp', axis=0, tiled=True)]
  transfers between devices with their start and end apart: 8 -> 10, of which waited for: 7 -> 9; matrix products, arithmetic and copies ran while one was open for 5% -> 6% of each run, Pallas kernels for 0% -> 0%
where the time goes in v1:
time: 542 us
  waiting for transfers between devices  388 us (72%)
  blocking collectives  88.8 us (16%)
  local copies, waits for them, and re-layouts  23.3 us (4%)
  matrix products  16.3 us (3%)
  between operations  14 us (3%)
  starting transfers between devices  6.73 us (1%)
    all_gather x1, waiting for transfers between devices, body(): lax.all_gather(value_weight, ('dp', 'mp'), axis=0, tiled=True)  141 us
    psum x1, waiting for transfers between devices, body(): llm_total = lax.psum(llm_part, ('dp', 'mp'))  94.7 us
    ppermute x2, waiting for transfers between devices, passed_along(): lax.ppermute(value, axis, [(source, source + steps) for source in range(f...  60 us
    all_to_all x1, blocking collectives, body(): lax.all_to_all(outgoing, ('dp', 'mp'), split_axis=1, concat_axis=1, tiled...  57.2 us
    ppermute x3, waiting for transfers between devices, switch_point(): b_now[h] = lax.ppermute(b_now[h + 1], chip_axis, sides)  50.8 us
    psum x1, waiting for transfers between devices, body(): enc_total = lax.psum(enc_part, 'dp')  38.8 us
    all_to_all x1, blocking collectives, body(): lax.all_to_all(reply_rows, ('dp', 'mp'), split_axis=1, concat_axis=1, til...  31.6 us
  transfers between devices with their start and end apart: 10, of which 9 were waited for; matrix products, arithmetic and copies ran while one was open for 6% of the time, Pallas kernels for 0%

profile of v1, /device:TPU:0, one launch (start us, length us, event | category | flops | bytes accessed | tf_op | source)
XLA Modules:
  0.0 541.7 jit_solution(866493241003923914)
XLA Ops:
  7.2 1.7 copy.53
  9.7 3.0 collective-permute-start
  12.7 16.8 %collective-permute-done = bf16[64,5120]{1,0:T(8,128)(2,1)S(1)} collective-permute-done((bf16[64,5120]{1,0:T(8,128)(2,1)}, bf16[64,5120]{1,0:T(8,128)(2,1)S(1)}, u32[]{:S(2)}, u32[]{:S(2)}) %collective-permute-start) | collective-permute-done | bytes 655392 | tf_op jit(solution)/shard_map/ppermute | solution.py:17
  31.6 18.4 %collective-permute-done.1 = bf16[64,5120]{1,0:T(8,128)(2,1)S(1)} collective-permute-done((bf16[64,5120]{1,0:T(8,128)(2,1)S(1)}, bf16[64,5120]{1,0:T(8,128)(2,1)S(1)}, u32[]{:S(2)}, u32[]{:S(2)}) %collective-permute-start.1) | collective-permute-done | bytes 655392 | tf_op jit(solution)/shard_map/ppermute | solution.py:17
  51.1 15.5 %collective-permute-done.2 = bf16[64,5120]{1,0:T(8,128)(2,1)S(1)} collective-permute-done((bf16[64,5120]{1,0:T(8,128)(2,1)S(1)}, bf16[64,5120]{1,0:T(8,128)(2,1)S(1)}, u32[]{:S(2)}, u32[]{:S(2)}) %collective-permute-start.2) | collective-permute-done | bytes 655392 | tf_op jit(solution)/shard_map/ppermute | solution.py:17
  73.7 15.3 %conditional.3 = (bf16[256,2048]{1,0:T(8,128)(2,1)S(1)}, bf16[256,64]{0,1:T(8,128)(2,1)}) conditional(s32[]{:T(128)} %convert_element_type.69, () %tuple.39, (s32[]{:T(128)}, s32[]{:T(128)}, bf16[512,5120]{1,0:T(8,128)(2,1)}, bf16[5120,2048]{1,0:T(8,128)(2,1)}, bf16[2048]{0:T(1024)(128)(2,1)S(1)}, /*index=5*/bf16[5120,64]{0,1:T(8,128)(2,1)}, ...), branch_computations={%region_3.4_spmd, %region_4.5_spmd.clone} | conditional | flops 5605181440 | bytes 32460980 | solution.py:86
  73.7 3.4 fusion.5
  78.3 10.7 %fusion.1 = bf16[256,2048]{1,0:T(8,128)(2,1)S(1)} fusion(f32[256,2048]{1,0:T(8,128)S(1)} %fusion.29, bf16[5120,2048]{1,0:T(8,128)(2,1)} %get-tuple-element.217, bf16[512,5120]{1,0:T(8,128)(2,1)} %get-tuple-element.213, s32[]{:T(128)S(6)} %select_n.78, f32[2048]{0:T(1024)S(1)} %convert_element_type.76), kind=kOutput, calls=%fused_computation.4 | convolution fusion | flops 5370281984 | bytes 26746884 | tf_op jit(solution)/shard_map/cond/branch_1_fun/dot_general | solution.py:74
  89.0 2.8 scatter_custom_fusion
  93.1 57.2 %all_to_all.10 = bf16[32,16,2048]{2,0,1:T(8,128)(2,1)} all-to-all(bf16[32,16,2048]{2,0,1:T(8,128)(2,1)S(1)} %copy.52), channel_id=1, replica_groups=mesh['grp'=2,'dp'=4,'mp'=4] {'dp','mp'}, dimensions={1} | all-to-all | bytes 4194304 | tf_op jit(solution)/shard_map/all_to_all | solution.py:94
  150.3 1.4 collective-permute-start.3
  151.7 3.8 collective-permute-done.3
  155.5 141.0 %all-gather.5.cloned.1.call-done = bf16[8192,1024]{1,0:T(8,128)(2,1)} async-done(((bf16[512,1024]{1,0:T(8,128)(2,1)}), bf16[8192,1024]{1,0:T(8,128)(2,1)}) %all-gather.5.cloned.1.call-update) | async-done | bytes 16777232 | tf_op jit(solution)/shard_map/all_gather | solution.py:99
  298.2 31.6 %all_to_all.11 = bf16[32,16,2048]{2,0,1:T(8,128)(2,1)} all-to-all(bf16[32,16,2048]{2,0,1:T(8,128)(2,1)S(1)} %copy.55), channel_id=1, replica_groups=mesh['grp'=2,'dp'=4,'mp'=4] {'dp','mp'}, dimensions={1} | all-to-all | bytes 4194304 | tf_op jit(solution)/shard_map/all_to_all | solution.py:153
  331.2 56.2 %collective-permute-done.4 = bf16[32,16,2048]{2,0,1:T(8,128)(2,1)S(1)} collective-permute-done((bf16[32,16,2048]{2,0,1:T(8,128)(2,1)}, bf16[32,16,2048]{2,0,1:T(8,128)(2,1)S(1)}, u32[]{:S(2)}, u32[]{:S(2)}) %collective-permute-start.4) | collective-permute-done | bytes 2097184 | tf_op jit(solution)/shard_map/ppermute | solution.py:29
  387.4 6.5 %conditional.5 = (f32[64,2048]{1,0:T(8,128)S(1)}) conditional(s32[]{:T(128)} %convert_element_type.69, () %tuple.38, (bf16[32,16,2048]{2,0,1:T(8,128)(2,1)S(1)}, s32[256]{0:T(256)S(1)}, s32[256]{0:T(256)S(1)}, bf16[256,64]{0,1:T(8,128)(2,1)}) %tuple.85), branch_computations={%region_11.12_spmd, %region_12.13_spmd} | conditional | flops 67111168 | bytes 16294948 | solution.py:164
  387.4 1.3 copy-done.3
  388.7 2.7 copy.56
  391.5 1.4 gather_fusion
  394.7 94.7 %all-reduce.6.cloned.1.call-done = f32[64,1024]{1,0:T(8,128)} async-done(((f32[64,1024]{1,0:T(8,128)}), f32[64,1024]{1,0:T(8,128)}) %all-reduce.6.cloned.1.call-update) | async-done | bytes 262160 | tf_op jit(solution)/shard_map/psum | solution.py:152
  490.4 38.8 %all-reduce.4.cloned.1.call-done = f32[64,2048]{1,0:T(8,128)} async-done(((f32[64,2048]{1,0:T(8,128)}), f32[64,2048]{1,0:T(8,128)}) %all-reduce.4.cloned.1.call-update) | async-done | bytes 524304 | tf_op jit(solution)/shard_map/psum | solution.py:165
  530.3 1.5 collective-permute-done.5
  532.0 1.7 slice_select_fusion.1
  533.6 1.6 slice_select_fusion.2
  (70 shorter events, 20.7 us)
Async XLA Ops:
  7.2 62.1 %copy-start.1 = (bf16[64,5120]{1,0:T(8,128)(2,1)S(1)}, bf16[64,5120]{1,0:T(8,128)(2,1)}, u32[]{:S(2)}) copy-start(bf16[64,5120]{1,0:T(8,128)(2,1)} %param.20) | copy-start | bytes 1966084
  7.2 144.5 %all-gather.3.cloned.1.call-start = ((), (), s32[]{:S(2)}) async-start(), calls=%async_computation.2 | async-start | bytes 2228224 | tf_op jit(solution)/shard_map/all_gather | solution.py:100
  8.9 287.6 %all-gather.5.cloned.1.call-start = ((), (), s32[]{:S(2)}) async-start(), calls=%async_computation.3 | async-start | bytes 17825792 | tf_op jit(solution)/shard_map/all_gather | solution.py:99
  9.7 479.8 %all-reduce.6.cloned.1.call-start = ((), (), s32[]{:S(2)}) async-start(), calls=%async_computation.5 | async-start | bytes 524288 | tf_op jit(solution)/shard_map/psum | solution.py:152
  9.7 19.9 %collective-permute-start = (bf16[64,5120]{1,0:T(8,128)(2,1)}, bf16[64,5120]{1,0:T(8,128)(2,1)S(1)}, u32[]{:S(2)}, u32[]{:S(2)}) collective-permute-start(bf16[64,5120]{1,0:T(8,128)(2,1)} %param.20), channel_id=1, source_target_pairs={{0,1},{1,2},{2,3},{3,0},{4,5},{5,6},{6,7},{7,4},{8,9},{9,10},{10,1... | collective-permute-start | bytes 1966088 | tf_op jit(solution)/shard_map/ppermute | solution.py:17
  29.6 20.5 %collective-permute-start.1 = (bf16[64,5120]{1,0:T(8,128)(2,1)S(1)}, bf16[64,5120]{1,0:T(8,128)(2,1)S(1)}, u32[]{:S(2)}, u32[]{:S(2)}) collective-permute-start(bf16[64,5120]{1,0:T(8,128)(2,1)S(1)} %collective-permute-done), channel_id=1, source_target_pairs={{0,1},{1,2},{2,3},{3,0},{4,5},{5,6},{6,7},{7,4},{8,9},{9,10},{10,1... | collective-permute-start | bytes 1966088 | tf_op jit(solution)/shard_map/ppermute | solution.py:17
  50.0 16.5 %collective-permute-start.2 = (bf16[64,5120]{1,0:T(8,128)(2,1)S(1)}, bf16[64,5120]{1,0:T(8,128)(2,1)S(1)}, u32[]{:S(2)}, u32[]{:S(2)}) collective-permute-start(bf16[64,5120]{1,0:T(8,128)(2,1)S(1)} %collective-permute-done.1), channel_id=1, source_target_pairs={{0,1},{1,2},{2,3},{3,0},{4,5},{5,6},{6,7},{7,4},{8,9},{9,10},{10,1... | collective-permute-start | bytes 1966088 | tf_op jit(solution)/shard_map/ppermute | solution.py:17
  68.3 5.4 copy-start.9
  68.3 5.4 copy-start.12
  91.8 204.7 %copy-start.7 = (bf16[64,1024]{1,0:T(8,128)(2,1)S(1)}, bf16[64,1024]{1,0:T(8,128)(2,1)}, u32[]{:S(2)}) copy-start(bf16[64,1024]{1,0:T(8,128)(2,1)} %param.30) | copy-start | bytes 393220
  91.8 204.7 %copy-start.8 = (bf16[160,1024]{1,0:T(8,128)(2,1)S(1)}, bf16[160,1024]{1,0:T(8,128)(2,1)}, u32[]{:S(2)}) copy-start(bf16[160,1024]{1,0:T(8,128)(2,1)} %param.31) | copy-start | bytes 983044
  91.9 204.7 %copy-start.10 = (bf16[8192]{0:T(1024)(128)(2,1)S(1)}, bf16[8192]{0:T(1024)(128)(2,1)}, u32[]{:S(2)}) copy-start(bf16[8192]{0:T(1024)(128)(2,1)} %param.26) | copy-start | bytes 49156
  91.9 204.7 %copy-start.11 = (s32[1024,1]{0,1:T(1,128)S(1)}, s32[1024,1]{0,1:T(1,128)}, u32[]{:S(2)}) copy-start(s32[1024,1]{0,1:T(1,128)} %param.32) | copy-start | bytes 12292
  91.9 204.7 %copy-start.13 = (bf16[1024]{0:T(1024)(128)(2,1)S(1)}, bf16[1024]{0:T(1024)(128)(2,1)}, u32[]{:S(2)}) copy-start(bf16[1024]{0:T(1024)(128)(2,1)} %param.28) | copy-start | bytes 6148
  150.3 5.3 collective-permute-start.3
  297.1 32.8 %copy-start.6 = (f32[64,1024]{1,0:T(8,128)}, f32[64,1024]{1,0:T(8,128)S(1)}, u32[]{:S(2)}) copy-start(f32[64,1024]{1,0:T(8,128)S(1)} %get-tuple-element.177) | copy-start | bytes 786436
  329.8 57.5 %collective-permute-start.4 = (bf16[32,16,2048]{2,0,1:T(8,128)(2,1)}, bf16[32,16,2048]{2,0,1:T(8,128)(2,1)S(1)}, u32[]{:S(2)}, u32[]{:S(2)}) collective-permute-start(bf16[32,16,2048]{2,0,1:T(8,128)(2,1)} %all_to_all.11), channel_id=1, source_target_pairs={{16,0},{17,1},{18,2},{19,3},{20,4},{21,5},{22,6},{23,7},{24,8},{25... | collective-permute-start | bytes 6291464 | tf_op jit(solution)/shard_map/ppermute | solution.py:29
  331.1 198.0 %all-reduce.4.cloned.1.call-start = ((), (), s32[]{:S(2)}) async-start(), calls=%async_computation.4 | async-start | bytes 1048576 | tf_op jit(solution)/shard_map/psum | solution.py:165
  387.4 1.3 copy-start.3
  393.9 0.8 copy-start.4
  530.2 1.6 collective-permute-start.5
Sparse Core Ops, SparseCore 0:
  11.3 68.5 all-gather.2
  82.7 213.7 all-gather.4
  331.3 158.1 all-reduce.5
  491.6 37.5 all-reduce.3
